TPU v7x, 32 devices: a whole 2x2x4 slice. The times are simulated.
32 devices in a mesh: design: 2 (over x), blk: 16 (over z, y, core).
Axes of the slice: x: 2, y: 2, z: 4, core: 2. Of those that a mesh axis runs over, the one named last changes fastest.
Arguments:
- right_side: float32 [6, 256, 1024], P(None, ('design', 'blk')), parts along dimension 1, may hold values from -6 to 6
- adjoint_start: float32 [6, 256, 1024], P(None, ('design', 'blk')), parts along dimension 1, may hold values from -3 to 3
- diag_inverse: float32 [6, 6, 256, 1024], P(None, None, ('design', 'blk')), parts along dimension 2
- face_jacobian: bfloat16 [4, 6, 6, 256, 1024], P(None, None, None, ('design', 'blk')), parts along dimension 3, may hold values from -0.25 to 0.25
- receptor_cell: int32 [32, 16, 16], P(('design', 'blk')), parts along dimension 0, may hold values from 0 to 8191
- donor_cell: int32 [32, 16, 4, 16], P(('design', 'blk')), parts along dimension 0, may hold values from 0 to 8191
- donor_weight: float32 [32, 16, 4, 16], P(('design', 'blk')), parts along dimension 0, may hold values from 0 to 1, as said below
- live_count: int32 [32, 16], P(('design', 'blk')), parts along dimension 0, may hold values from 0 to 16, as said below
Outputs:
- adjoint: float32 [6, 256, 1024], P(None, ('design', 'blk')), parts along dimension 1
- correction_norms: float32 [4], P('design'), parts along dimension 0
There are 2 independent parts, one for each index of `design`. A program takes and returns all parts, laid end to end along the dimension named above; each array names one. Nothing has to cross between parts.
Inputs may be any that keep to these rules, and one draw needn't show every extreme that they name: live_count[s, d] counts the leading live slots of list (s, d); in every draw some partition d has 16 live slots from every source s. `donor_weight`: the four weights of each slot are positive and sum to 1.
All inputs are finite; a program needn't handle non-finite values.
Results may differ from a plain program's by a relative error of at most 0.0003.
Values sent between devices are 32-bit elements; how exact they have to be, the bound alone decides.
A program may use at most 64 MiB of HBM per device.

v0:
```python
import math

import jax
import jax.numpy as jnp
from jax import lax
from jax.sharding import PartitionSpec as P

SWEEPS = 2


def padded_2(block, sides, width):
    for axis, dim in sides:
        count = lax.axis_size(axis)
        forward = [(i, i + 1) for i in range(count - 1)]
        backward = [(target, source) for source, target in forward]
        low = lax.ppermute(
            lax.slice_in_dim(block, block.shape[dim] - width, None, axis=dim), axis, forward
        )
        high = lax.ppermute(lax.slice_in_dim(block, 0, width, axis=dim), axis, backward)
        block = jnp.concatenate([low, block, high], axis=dim)
    return block


def group_count(parts, rows_each):
    best = 1
    for count in range(1, parts + 1):
        if parts % count == 0 and count * rows_each <= 2048:
            best = count
    return best


def split_index(index, width, blocks):
    upper = index // width
    lower = index - upper * width
    block_hot = (upper[:, None] == jnp.arange(blocks, dtype=jnp.int32)[None, :]).astype(jnp.float32)
    offset_hot = (lower[:, None] == jnp.arange(width, dtype=jnp.int32)[None, :]).astype(jnp.float32)
    return (block_hot, offset_hot)


def pick_cells(field, index, rows_each):
    nvar, cells = field.shape
    parts = index.shape[0] // rows_each
    width = math.gcd(cells, 128)
    blocks = cells // width
    shaped = field.reshape(nvar, blocks, width)
    members = group_count(parts, rows_each)
    grouped = index.reshape(parts // members, members * rows_each)

    def pick_one_group(rows_index):
        block_hot, offset_hot = split_index(rows_index, width, blocks)
        picked = jnp.einsum("tb,abo->tao", block_hot, shaped, precision=lax.Precision.HIGHEST)
        return jnp.sum(picked * offset_hot[:, None, :], axis=2)

    gathered = lax.map(pick_one_group, grouped)
    return jnp.transpose(gathered, (2, 0, 1)).reshape(nvar, -1)


def spread_cells(terms, index, cells, rows_each):
    nvar = terms.shape[0]
    parts = index.shape[0] // rows_each
    width = math.gcd(cells, 128)
    blocks = cells // width
    members = group_count(parts, rows_each)
    groups = parts // members
    grouped_index = index.reshape(groups, members * rows_each)
    grouped_terms = jnp.transpose(terms.reshape(nvar, groups, members * rows_each), (1, 0, 2))

    def spread_one_group(total, pieces):
        rows_index, rows_terms = pieces
        block_hot, offset_hot = split_index(rows_index, width, blocks)
        weighted = rows_terms[:, :, None] * block_hot[None]
        added = jnp.einsum("atb,to->abo", weighted, offset_hot, precision=lax.Precision.HIGHEST)
        return (total + added, None)

    start = jnp.zeros((nvar, blocks, width), jnp.float32)
    total, unused = lax.scan(spread_one_group, start, (grouped_index, grouped_terms))
    return total.reshape(nvar, cells)


def face_coupling(psi, face_jacobian):
    padded = padded_2(psi, (("blk", 1),), 1)
    widened = jnp.pad(psi, ((0, 0), (0, 0), (1, 1)))
    sides = (padded[:, :-2, :], padded[:, 2:, :], widened[:, :, :-2], widened[:, :, 2:])
    coupled = jnp.zeros(psi.shape, jnp.float32)
    for face in range(4):
        coupled = coupled + jnp.einsum(
            "abij,bij->aij",
            face_jacobian[face].astype(jnp.float32),
            sides[face],
            precision=lax.Precision.HIGHEST,
        )
    return coupled


def body(
    right_side,
    adjoint_start,
    diag_inverse,
    face_jacobian,
    receptor_cell,
    donor_cell,
    donor_weight,
    live_count,
):
    nvar, rows, cols = right_side.shape
    cells = rows * cols
    slots = receptor_cell.shape[2]
    live = (jnp.arange(slots, dtype=jnp.int32)[None, :] < live_count[0][:, None]).astype(
        jnp.float32
    )
    targets = lax.all_to_all(donor_cell[0], "blk", split_axis=0, concat_axis=0, tiled=True).reshape(
        -1
    )
    sources = receptor_cell[0].reshape(-1)
    rhs_local = jnp.sum(right_side * right_side)
    psi = adjoint_start
    partials = []
    for sweep in range(SWEEPS):
        picked = pick_cells(psi.reshape(nvar, cells), sources, slots)
        values = picked.reshape(nvar, -1, slots) * live[None]
        weighted = values[:, :, None, :] * donor_weight[0][None]
        terms = lax.all_to_all(weighted, "blk", split_axis=1, concat_axis=1, tiled=True)
        spread = spread_cells(terms.reshape(nvar, -1), targets, cells, 4 * slots)
        coupled = face_coupling(psi, face_jacobian)
        source = right_side - coupled + spread.reshape(psi.shape)
        new = jnp.einsum("abij,bij->aij", diag_inverse, source, precision=lax.Precision.HIGHEST)
        change = new - psi
        partial_sq = jnp.sum(change * change)
        partials.append(partial_sq)
        psi = new
    totals = lax.psum(jnp.stack([rhs_local] + partials), "blk")
    result_norms = jnp.sqrt(totals[1:] / (totals[0] + 1e-06))
    return (psi, result_norms)


def solution(mesh):
    return jax.shard_map(
        body,
        mesh=mesh,
        in_specs=(
            P(None, ("design", "blk"), None),
            P(None, ("design", "blk"), None),
            P(None, None, ("design", "blk"), None),
            P(None, None, None, ("design", "blk"), None),
            P(("design", "blk"), None, None),
            P(("design", "blk"), None, None, None),
            P(("design", "blk"), None, None, None),
            P(("design", "blk"), None),
        ),
        out_specs=(P(None, ("design", "blk"), None), P("design")),
        check_vma=False,
    )
```

profile of v0, /device:TPU:0, one launch (start us, length us, event | category | flops | bytes accessed | tf_op | source)
XLA Modules:
  0.0 102.9 jit_solution(15937769331518278682)
XLA Ops:
  0.6 0.0 copy-start.4
  0.6 0.0 copy-start.12
  0.7 7.6 %all-to-all-start.1 = ((s32[16,4,16]{2,1,0:T(4,128)}), s32[16,4,16]{2,1,0:T(4,128)S(1)}, u32[]{:S(2)}, u32[]{:S(2)}) async-start(s32[16,4,16]{2,1,0:T(4,128)} %bitcast.113), calls=%async_computation.1 | async-start | bytes 65536 | tf_op jit(solution)/shard_map/all_to_all | solution.py:111
  8.2 1.1 %fusion.46 = (f32[6,1,1024]{2,1,0:T(1,128)S(1)}, f32[6,1,1024]{2,1,0:T(1,128)S(1)}) fusion(f32[6,8,1024]{2,1,0:T(8,128)} %param.9), kind=kLoop, calls=%fused_computation.89 | loop fusion | bytes 98304 | tf_op jit(solution)/shard_map/slice | solution.py:17
  9.3 2.3 %collective-permute-start = (f32[6,1,1024]{2,1,0:T(1,128)S(1)}, f32[6,1,1024]{2,1,0:T(1,128)S(1)}, u32[]{:S(2)}, u32[]{:S(2)}) collective-permute-start(f32[6,1,1024]{2,1,0:T(1,128)S(1)} %get-tuple-element.74), channel_id=1, source_target_pairs={{0,1},{1,2},{2,3},{3,4},{4,5},{5,6},{6,7},{7,8},{8,9},{9,10},{10,1... | collective-permute-start | bytes 73736 | tf_op jit(solution)/shard_map/ppermute | solution.py:16
  11.6 1.3 %collective-permute-start.1 = (f32[6,1,1024]{2,1,0:T(1,128)S(1)}, f32[6,1,1024]{2,1,0:T(1,128)S(1)}, u32[]{:S(2)}, u32[]{:S(2)}) collective-permute-start(f32[6,1,1024]{2,1,0:T(1,128)S(1)} %get-tuple-element.75), channel_id=1, source_target_pairs={{1,0},{2,1},{3,2},{4,3},{5,4},{6,5},{7,6},{8,7},{9,8},{10,9},{11,1... | collective-permute-start | bytes 73736 | tf_op jit(solution)/shard_map/ppermute | solution.py:19
  12.9 1.0 reshape_reshape.20
  13.9 0.8 squeeze.43
  14.7 0.7 fusion.42
  15.4 0.0 copy-start.13
  15.4 0.0 copy-start
  15.4 0.5 fusion.4
  16.0 0.1 copy-done.13
  16.1 0.1 reshape_reshape.21
  16.2 0.8 reshape.189
  17.0 0.0 all-to-all-done.1
  17.0 8.0 %all-to-all-start = ((f32[16,1,384]{2,1,0:T(1,128)}), f32[16,1,384]{2,1,0:T(1,128)S(1)}, u32[]{:S(2)}, u32[]{:S(2)}) async-start(f32[16,1,384]{2,1,0:T(1,128)} %reshape.189), calls=%async_computation | async-start | bytes 49152 | tf_op jit(solution)/shard_map/all_to_all | solution.py:122
  25.0 0.1 squeeze.45
  25.1 0.7 fusion.23
  25.8 0.0 collective-permute-done
  25.8 0.0 collective-permute-done.1
  25.8 0.2 fusion.24
  26.0 0.0 copy-done.16
  26.0 1.4 %fusion.8 = (f32[8,1024,6]{1,0,2:T(8,128)}, f32[8,1024,6]{1,0,2:T(8,128)}, f32[8,1024,6]{1,0,2:T(8,128)}, f32[8,1024,6]{1,0,2:T(8,128)}) fusion(f32[8,1024,6]{1,0,2:T(8,128)S(1)} %get-tuple-element.73, bf16[4,6,6,8,1024]{4,3,2,1,0:T(8,128)(2,1)S(1)} %copy-done, f32[8,1024,6]{1,0,2:T(8,128)S(1)} %get-tuple-element.72, ...), kind=kLoop, calls=%fused_computation.18 | loop fusion | flops 3342336 | bytes 3932160 | tf_op jit(solution)/shard_map/abij,bij->aij/dot_general | solution.py:86
  27.5 4.1 %all-to-all-done = f32[16,1,384]{2,1,0:T(1,128)S(1)} async-done(((f32[16,1,384]{2,1,0:T(1,128)}), f32[16,1,384]{2,1,0:T(1,128)S(1)}, u32[]{:S(2)}, u32[]{:S(2)}) %all-to-all-start) | async-done | bytes 24608 | tf_op jit(solution)/shard_map/all_to_all | solution.py:122
  31.6 0.5 broadcast.186
  32.1 0.7 reduce.20
  32.8 0.2 reshape.190
  33.0 0.8 mul.150
  33.8 2.7 %fusion.2 = f32[6,64,128]{2,1,0:T(8,128)} fusion(f32[1024,64]{0,1:T(8,128)} %fusion.23, f32[6,1024]{1,0:T(8,128)} %mul.150, s32[1024]{0:T(1024)S(1)} %get-tuple-element.76), kind=kOutput, calls=%fused_computation.2 | convolution fusion | flops 604504064 | bytes 487424 | tf_op jit(solution)/shard_map/while/body/eval_jaxpr/atb,to->abo/dot_general | solution.py:72
  36.5 1.6 %reshape_reshape.22 = f32[6,8,1024]{2,1,0:T(8,128)} reshape(f32[6,64,128]{2,1,0:T(8,128)} %fusion.2) | data formatting | bytes 393216 | tf_op jit(solution)/shard_map/reshape;reshape | solution.py:125
  38.2 2.0 %multiply_reduce_fusion.4 = (f32[]{:T(128)}, f32[8,1024,6]{1,0,2:T(8,128)S(1)}) fusion(f32[6,8,1024]{2,1,0:T(8,128)} %param.8, f32[6,8,1024]{2,1,0:T(8,128)} %reshape_reshape.22, f32[8,1024,6]{1,0,2:T(8,128)} %get-tuple-element.48, f32[8,1024,6]{1,0,2:T(8,128)} %get-tuple-element.49, f32[8,1024,6]{1,0,2:T(8,128)} %get-tuple-element.43, ...), kind=kLoop, calls=%fused_computation.60 | loop fusion | flops 344063 | bytes 1376260 | tf_op jit(solution)/shard_map/reduce_sum | solution.py:115
  40.1 0.1 multiply_reduce_fusion.1
  40.3 0.0 copy-start.2
  40.3 0.7 copy-done.2
  40.9 0.6 fusion.45
  41.6 1.6 %reshape_reshape.23 = f32[6,64,128]{2,1,0:T(8,128)} reshape(f32[6,8,1024]{2,1,0:T(8,128)} %bitcast.106) | data formatting | bytes 393216 | tf_op jit(solution)/shard_map/reshape;reshape | solution.py:45
  43.2 2.2 %collective-permute-start.2 = (f32[6,1,1024]{2,1,0:T(1,128)}, f32[6,1,1024]{2,1,0:T(1,128)}, u32[]{:S(2)}, u32[]{:S(2)}) collective-permute-start(f32[6,1,1024]{2,1,0:T(1,128)} %get-tuple-element.68), channel_id=1, source_target_pairs={{0,1},{1,2},{2,3},{3,4},{4,5},{5,6},{6,7},{7,8},{8,9},{9,10},{10,1... | collective-permute-start | bytes 73736 | tf_op jit(solution)/shard_map/ppermute | solution.py:16
  45.4 1.3 %collective-permute-start.3 = (f32[6,1,1024]{2,1,0:T(1,128)}, f32[6,1,1024]{2,1,0:T(1,128)}, u32[]{:S(2)}, u32[]{:S(2)}) collective-permute-start(f32[6,1,1024]{2,1,0:T(1,128)} %get-tuple-element.69), channel_id=1, source_target_pairs={{1,0},{2,1},{3,2},{4,3},{5,4},{6,5},{7,6},{8,7},{9,8},{10,9},{11,1... | collective-permute-start | bytes 73736 | tf_op jit(solution)/shard_map/ppermute | solution.py:19
  46.7 1.5 %fusion.5 = f32[256,6]{0,1:T(8,128)S(1)} fusion(f32[6,64,128]{2,1,0:T(8,128)} %reshape_reshape.23, f32[256,128]{0,1:T(8,128)} %copy-done.13, s32[256]{0:T(256)} %copy-done.16), kind=kOutput, calls=%fused_computation.15 | convolution fusion | flops 151403008 | bytes 334848 | tf_op jit(solution)/shard_map/while/body/eval_jaxpr/tb,abo->tao/dot_general | solution.py:51
  48.3 0.7 reshape_reshape.24
  49.0 0.8 broadcast_multiply_fusion.2
  49.8 1.5 %fusion.48 = f32[16,6,4,16]{3,2,1,0:T(4,128)} fusion(f32[16,4,16]{2,1,0:T(4,128)} %bitcast.111, f32[6,16,16]{2,0,1:T(8,128)S(1)} %copy.14), kind=kLoop, calls=%fused_computation.91 | loop fusion | flops 6144 | bytes 34816
  51.3 1.7 %reshape.191 = f32[16,1,384]{2,1,0:T(1,128)} reshape(f32[16,6,4,16]{3,2,1,0:T(4,128)} %fusion.48) | data formatting | bytes 49152
  53.0 4.9 %all-to-all-start.2 = ((f32[16,1,384]{2,1,0:T(1,128)}), f32[16,1,384]{2,1,0:T(1,128)}, u32[]{:S(2)}, u32[]{:S(2)}) async-start(f32[16,1,384]{2,1,0:T(1,128)} %reshape.191), calls=%async_computation.2 | async-start | bytes 49152 | tf_op jit(solution)/shard_map/all_to_all | solution.py:122
  57.9 0.0 collective-permute-done.2
  57.9 0.0 collective-permute-done.3
  57.9 1.4 %fusion.27 = (f32[8,1024,6]{1,0,2:T(8,128)S(1)}, f32[8,1024,6]{1,0,2:T(8,128)S(1)}, f32[8,1024,6]{1,0,2:T(8,128)S(1)}, f32[8,1024,6]{1,0,2:T(8,128)S(1)}) fusion(f32[6,8,1024]{2,1,0:T(8,128)} %bitcast.107, f32[6,1,1024]{2,1,0:T(1,128)} %collective-permute-done.2, f32[6,1,1024]{2,1,0:T(1,128)} %collective-permute-done.3), kind=kLoop, calls=%fused_computation.43 | loop fusion | flops 98304 | bytes 1032192
  59.3 1.4 %fusion.9 = (f32[8,1024,6]{1,0,2:T(8,128)}, f32[8,1024,6]{1,0,2:T(8,128)}, f32[8,1024,6]{1,0,2:T(8,128)}, f32[8,1024,6]{1,0,2:T(8,128)}) fusion(f32[8,1024,6]{1,0,2:T(8,128)S(1)} %get-tuple-element.67, bf16[4,6,6,8,1024]{4,3,2,1,0:T(8,128)(2,1)S(1)} %copy-done, f32[8,1024,6]{1,0,2:T(8,128)S(1)} %get-tuple-element.66, ...), kind=kLoop, calls=%fused_computation.19 | loop fusion | flops 3342336 | bytes 3932160 | tf_op jit(solution)/shard_map/abij,bij->aij/dot_general | solution.py:86
  60.8 3.7 %all-to-all-done.2 = f32[16,1,384]{2,1,0:T(1,128)} async-done(((f32[16,1,384]{2,1,0:T(1,128)}), f32[16,1,384]{2,1,0:T(1,128)}, u32[]{:S(2)}, u32[]{:S(2)}) %all-to-all-start.2) | async-done | bytes 24608 | tf_op jit(solution)/shard_map/all_to_all | solution.py:122
  64.5 1.4 %reduce.21 = f32[16,384]{1,0:T(8,128)S(1)} reduce(f32[16,1,384]{2,1,0:T(1,128)} %all-to-all-done.2, f32[]{:T(128)} %broadcast.186), dimensions={1}, to_apply=%all_to_all.11.reduce_sub_computation | reduce | bytes 49156 | tf_op jit(solution)/shard_map/all_to_all | solution.py:122
  66.0 0.2 reshape.192
  66.2 0.2 mul.159
  66.4 1.9 %fusion = f32[6,64,128]{2,1,0:T(8,128)S(1)} fusion(f32[6,1024]{1,0:T(8,128)S(1)} %mul.159, f32[1024,64]{0,1:T(8,128)} %fusion.23, s32[1024]{0:T(1024)S(1)} %copy-done.15), kind=kOutput, calls=%fused_computation | convolution fusion | flops 604504064 | bytes 487424 | tf_op jit(solution)/shard_map/while/body/eval_jaxpr/atb,to->abo/dot_general | solution.py:72
  68.4 0.0 copy-start.3
  68.4 0.0 copy-start.5
  68.4 0.1 fusion.33
  68.5 0.1 multiply_reduce_fusion
  68.6 0.7 copy-done.3
  69.3 0.1 copy-done.5
  69.4 0.8 multiply_reduce_fusion.3
  70.2 2.0 %pad_maximum_fusion.4 = f32[3]{0:T(128)S(1)} fusion(f32[1]{0:T(128)} %bitcast.49, f32[1]{0:T(128)} %bitcast.48, f32[1]{0:T(128)} %bitcast.47), kind=kLoop, calls=%fused_computation.86 | loop fusion | flops 6 | bytes 24 | tf_op jit(solution)/shard_map/stack | solution.py:131
  72.1 30.1 %psum.7 = f32[3]{0:T(128)S(1)} all-reduce(f32[3]{0:T(128)S(1)} %pad_maximum_fusion.4), channel_id=1, replica_groups=mesh['design'=2,'blk'=16] {'blk'}, use_global_device_ids=true, to_apply=%region_5.6 | all-reduce | flops 3 | bytes 24 | tf_op jit(solution)/shard_map/psum | solution.py:131
  102.3 0.6 divide_sqrt_fusion
  (32 shorter events, 0.3 us)
Async XLA Ops:
  0.6 25.2 %copy-start.4 = (f32[6,8,1024]{2,1,0:T(8,128)S(1)}, f32[6,8,1024]{2,1,0:T(8,128)}, u32[]{:S(2)}) copy-start(f32[6,8,1024]{2,1,0:T(8,128)} %param.9) | copy-start | bytes 589828
  0.6 15.5 %copy-start.12 = (f32[1,16,4,16]{3,2,1,0:T(4,128)S(1)}, f32[1,16,4,16]{3,2,1,0:T(4,128)}, u32[]{:S(2)}) copy-start(f32[1,16,4,16]{3,2,1,0:T(4,128)} %param.14) | copy-start | bytes 12292
  0.7 16.4 %all-to-all-start.1 = ((s32[16,4,16]{2,1,0:T(4,128)}), s32[16,4,16]{2,1,0:T(4,128)S(1)}, u32[]{:S(2)}, u32[]{:S(2)}) async-start(s32[16,4,16]{2,1,0:T(4,128)} %bitcast.113), calls=%async_computation.1 | async-start | bytes 65536 | tf_op jit(solution)/shard_map/all_to_all | solution.py:111
  9.3 16.5 %collective-permute-start = (f32[6,1,1024]{2,1,0:T(1,128)S(1)}, f32[6,1,1024]{2,1,0:T(1,128)S(1)}, u32[]{:S(2)}, u32[]{:S(2)}) collective-permute-start(f32[6,1,1024]{2,1,0:T(1,128)S(1)} %get-tuple-element.74), channel_id=1, source_target_pairs={{0,1},{1,2},{2,3},{3,4},{4,5},{5,6},{6,7},{7,8},{8,9},{9,10},{10,1... | collective-permute-start | bytes 73736 | tf_op jit(solution)/shard_map/ppermute | solution.py:16
  11.6 14.2 %collective-permute-start.1 = (f32[6,1,1024]{2,1,0:T(1,128)S(1)}, f32[6,1,1024]{2,1,0:T(1,128)S(1)}, u32[]{:S(2)}, u32[]{:S(2)}) collective-permute-start(f32[6,1,1024]{2,1,0:T(1,128)S(1)} %get-tuple-element.75), channel_id=1, source_target_pairs={{1,0},{2,1},{3,2},{4,3},{5,4},{6,5},{7,6},{8,7},{9,8},{10,9},{11,1... | collective-permute-start | bytes 73736 | tf_op jit(solution)/shard_map/ppermute | solution.py:19
  14.7 11.4 %copy-start.16 = (s32[256]{0:T(256)}, s32[256]{0:T(256)S(1)}, u32[]{:S(2)}) copy-start(s32[256]{0:T(256)S(1)} %get-tuple-element.57) | copy-start | bytes 3076
  15.4 0.6 copy-start.13
  15.4 10.6 %copy-start = (bf16[4,6,6,8,1024]{4,3,2,1,0:T(8,128)(2,1)S(1)}, bf16[4,6,6,8,1024]{4,3,2,1,0:T(8,128)(2,1)}, u32[]{:S(2)}) copy-start(bf16[4,6,6,8,1024]{4,3,2,1,0:T(8,128)(2,1)} %param.11) | copy-start | bytes 7077892
  17.0 14.5 %all-to-all-start = ((f32[16,1,384]{2,1,0:T(1,128)}), f32[16,1,384]{2,1,0:T(1,128)S(1)}, u32[]{:S(2)}, u32[]{:S(2)}) async-start(f32[16,1,384]{2,1,0:T(1,128)} %reshape.189), calls=%async_computation | async-start | bytes 49152 | tf_op jit(solution)/shard_map/all_to_all | solution.py:122
  25.1 8.7 %copy-start.14 = (s32[1024]{0:T(1024)}, s32[1024]{0:T(1024)S(1)}, u32[]{:S(2)}) copy-start(s32[1024]{0:T(1024)S(1)} %get-tuple-element.76) | copy-start | bytes 12292
  33.8 6.3 %copy-start.1 = (f32[6,6,8,1024]{3,2,1,0:T(8,128)S(1)}, f32[6,6,8,1024]{3,2,1,0:T(8,128)}, u32[]{:S(2)}) copy-start(f32[6,6,8,1024]{3,2,1,0:T(8,128)} %param.10) | copy-start | bytes 3538948
  40.3 0.7 copy-start.2
  43.2 14.7 %collective-permute-start.2 = (f32[6,1,1024]{2,1,0:T(1,128)}, f32[6,1,1024]{2,1,0:T(1,128)}, u32[]{:S(2)}, u32[]{:S(2)}) collective-permute-start(f32[6,1,1024]{2,1,0:T(1,128)} %get-tuple-element.68), channel_id=1, source_target_pairs={{0,1},{1,2},{2,3},{3,4},{4,5},{5,6},{6,7},{7,8},{8,9},{9,10},{10,1... | collective-permute-start | bytes 73736 | tf_op jit(solution)/shard_map/ppermute | solution.py:16
  45.4 12.5 %collective-permute-start.3 = (f32[6,1,1024]{2,1,0:T(1,128)}, f32[6,1,1024]{2,1,0:T(1,128)}, u32[]{:S(2)}, u32[]{:S(2)}) collective-permute-start(f32[6,1,1024]{2,1,0:T(1,128)} %get-tuple-element.69), channel_id=1, source_target_pairs={{1,0},{2,1},{3,2},{4,3},{5,4},{6,5},{7,6},{8,7},{9,8},{10,9},{11,1... | collective-permute-start | bytes 73736 | tf_op jit(solution)/shard_map/ppermute | solution.py:19
  53.0 11.5 %all-to-all-start.2 = ((f32[16,1,384]{2,1,0:T(1,128)}), f32[16,1,384]{2,1,0:T(1,128)}, u32[]{:S(2)}, u32[]{:S(2)}) async-start(f32[16,1,384]{2,1,0:T(1,128)} %reshape.191), calls=%async_computation.2 | async-start | bytes 49152 | tf_op jit(solution)/shard_map/all_to_all | solution.py:122
  59.3 7.0 %copy-start.15 = (s32[1024]{0:T(1024)S(1)}, s32[1024]{0:T(1024)}, u32[]{:S(2)}) copy-start(s32[1024]{0:T(1024)} %copy-done.14) | copy-start | bytes 12292
  60.8 7.6 %copy-start.7 = (f32[6,8,1024]{2,1,0:T(8,128)S(1)}, f32[6,8,1024]{2,1,0:T(8,128)}, u32[]{:S(2)}) copy-start(f32[6,8,1024]{2,1,0:T(8,128)} %param.8) | copy-start | bytes 589828
  60.8 7.6 %copy-start.8 = (f32[8,1024,6]{1,0,2:T(8,128)S(1)}, f32[8,1024,6]{1,0,2:T(8,128)}, u32[]{:S(2)}) copy-start(f32[8,1024,6]{1,0,2:T(8,128)} %get-tuple-element.34) | copy-start | bytes 589828
  60.8 7.6 %copy-start.9 = (f32[8,1024,6]{1,0,2:T(8,128)S(1)}, f32[8,1024,6]{1,0,2:T(8,128)}, u32[]{:S(2)}) copy-start(f32[8,1024,6]{1,0,2:T(8,128)} %get-tuple-element.35) | copy-start | bytes 589828
  60.8 7.6 %copy-start.10 = (f32[8,1024,6]{1,0,2:T(8,128)S(1)}, f32[8,1024,6]{1,0,2:T(8,128)}, u32[]{:S(2)}) copy-start(f32[8,1024,6]{1,0,2:T(8,128)} %get-tuple-element.40) | copy-start | bytes 589828
  60.8 7.6 %copy-start.11 = (f32[8,1024,6]{1,0,2:T(8,128)S(1)}, f32[8,1024,6]{1,0,2:T(8,128)}, u32[]{:S(2)}) copy-start(f32[8,1024,6]{1,0,2:T(8,128)} %get-tuple-element.41) | copy-start | bytes 589828
  68.4 0.9 copy-start.3
  68.4 1.0 copy-start.5
  69.4 33.5 %copy-start.6 = (f32[8,1024,6]{1,0,2:T(8,128)}, f32[8,1024,6]{1,0,2:T(8,128)S(1)}, u32[]{:S(2)}) copy-start(f32[8,1024,6]{1,0,2:T(8,128)S(1)} %multiply_reduce_fusion) | copy-start | bytes 589828
where the time goes:
time: 104 us; the launch traced here: 103 us
  blocking collectives  30.1 us (29%)
  starting transfers between devices  27.5 us (26%)
  other arithmetic  16 us (15%)
  local copies, waits for them, and re-layouts  13.7 us (13%)
  waiting for transfers between devices  7.82 us (8%)
  matrix products  6.72 us (6%)
  between operations  1.06 us (1%)
    psum x1, blocking collectives, body(): totals = lax.psum(jnp.stack([rhs_local] + partials), 'blk')  30.1 us
    all_to_all x2, starting transfers between devices, body(): lax.all_to_all(weighted, 'blk', split_axis=1, concat_axis=1, tiled=True)  12.9 us
    all_to_all x2, waiting for transfers between devices, body(): lax.all_to_all(weighted, 'blk', split_axis=1, concat_axis=1, tiled=True)  7.81 us
    all_to_all x1, starting transfers between devices, body(): lax.all_to_all(donor_cell[0], 'blk', split_axis=0, concat_axis=0, tiled=T...  7.56 us
    dot_general x2, matrix products, spread_one_group(): jnp.einsum('atb,to->abo', weighted, offset_hot, precision=lax.Precision.H...  4.65 us
    ppermute x2, starting transfers between devices, padded_2(): lax.ppermute(lax.slice_in_dim(block, block.shape[dim] - width, None, axis...  4.52 us
    unnamed x38, local copies, waits for them, and re-layouts  4.45 us
    unnamed x5, other arithmetic  3.18 us
  transfers between devices with their start and end apart: 7, of which 2 were waited for; matrix products, arithmetic and copies ran while one was open for 16% of the time, Pallas kernels for 0%

commit v1 on v0

v1 whole, which is shorter than its diff:
```python
import functools

import jax
import jax.numpy as jnp
from jax import lax
from jax.experimental import pallas as pl
from jax.experimental.pallas import tpu as pltpu
from jax.sharding import PartitionSpec as P

SWEEPS = 2
LANES = 128
MESH = pl.DeviceIdType.MESH
F32 = jnp.float32
BF16 = jnp.bfloat16


def two_pieces(x):
    high = x.astype(BF16)
    low = (x - high.astype(F32)).astype(BF16)
    return high, low


def wait_bytes(ref, sem):
    pltpu.make_async_copy(ref, ref, sem).wait()


def kernel(
    n,
    live_s,
    rhs_h,
    psi_h,
    dinv_h,
    jac_h,
    rec_h,
    don_h,
    wgt_h,
    out_ref,
    norm_s,
    rhs,
    psi0,
    psi1,
    dinv,
    jac,
    rec,
    don,
    wgt,
    acc,
    near,
    recpad,
    stage,
    stage_in,
    vsend,
    vrecv,
    hsend,
    hrecv,
    nsend,
    nrecv,
    pick_hot,
    pick_block,
    add_hot,
    add_block,
    lhs,
    weights,
    local_sem,
    stage_sem,
    v_sem,
    h_sem,
    n_sem,
):
    nvar, rows, cols = psi0.shape
    slots = rec.shape[1]
    donors = don.shape[1]
    lists = n * slots
    per = LANES // slots
    tiles = lists // LANES
    width = pick_hot.shape[0]
    strips = cols // width
    blocks = rows * strips
    full = nvar * blocks
    me = lax.axis_index("blk")
    design = lax.axis_index("design")

    barrier = pltpu.get_barrier_semaphore()

    def greet(j, carry):
        pl.semaphore_signal(
            barrier, inc=1, device_id=(design, lax.rem(me + j, n)), device_id_type=MESH
        )
        return carry

    lax.fori_loop(1, n, greet, 0)

    loads = []
    for k, (src, dst) in enumerate(
        (
            (psi_h, psi0),
            (rec_h.at[0], rec),
            (don_h.at[0], don),
            (wgt_h.at[0], wgt),
            (jac_h, jac),
            (rhs_h, rhs),
            (dinv_h, dinv),
        )
    ):
        copy = pltpu.make_async_copy(src, dst, local_sem.at[k])
        copy.start()
        loads.append(copy)

    def split_cell(row):
        i = jnp.floor((row + 0.5) * (1.0 / cols))
        j = row - i * cols
        q = jnp.floor((j + 0.5) * (1.0 / width))
        return (q * rows + i).astype(jnp.int32), (j - q * width).astype(jnp.int32)

    def to_all(source_of, dest_ref, send_sem, recv_sem):
        def send(j, carry):
            dest = lax.rem(me + j, n)
            pltpu.make_async_remote_copy(
                src_ref=source_of(dest),
                dst_ref=dest_ref.at[me],
                send_sem=send_sem,
                recv_sem=recv_sem,
                device_id=(design, dest),
                device_id_type=MESH,
            ).start()
            return carry

        lax.fori_loop(1, n, send, 0)

    def halo_copies(sweep):
        below = lax.rem(me + n - 1, n)
        above = lax.rem(me + 1, n)
        return [
            pltpu.make_async_remote_copy(
                src_ref=hsend.at[sweep, side],
                dst_ref=hrecv.at[sweep, side],
                send_sem=h_sem.at[sweep, side, 0],
                recv_sem=h_sem.at[sweep, side, 1],
                device_id=(design, target),
                device_id_type=MESH,
            )
            for side, target in ((0, above), (1, below))
        ]

    def assemble(tile_of):
        parts = []
        for h in range(tiles):
            total = None
            for g in range(per):
                tile = tile_of(h * per + g)
                if g:
                    tile = pltpu.roll(tile, g * slots, 1)
                total = tile if total is None else total + tile
            parts.append(total)
        return parts

    def put_halo(sweep, psi):
        hsend[sweep, 0] = psi[:, rows - 1, :]
        hsend[sweep, 1] = psi[:, 0, :]

    def pick(sweep, psi):
        x = jnp.concatenate(
            [psi[a, :, q * width : (q + 1) * width] for a in range(nvar) for q in range(strips)],
            axis=0,
        )
        high, low = two_pieces(x)
        got = jnp.dot(
            jnp.concatenate([high, low], axis=0), pick_hot[...], preferred_element_type=F32
        )
        got = (got[:full] + got[full:]).reshape(nvar, blocks, lists)
        got = jnp.sum(got * pick_block[...][None], axis=1)
        for h in range(tiles):
            vsend[sweep, h, 0:nvar, :] = got[:, h * LANES : (h + 1) * LANES]

    stage[...] = jnp.zeros(stage.shape, F32)
    recpad[...] = jnp.zeros(recpad.shape, F32)
    vsend[...] = jnp.zeros(vsend.shape, F32)
    loads[1].wait()
    recpad[:, 0:slots] = rec[...].astype(F32)
    loads[2].wait()
    loads[3].wait()
    slot_id = lax.broadcasted_iota(jnp.int32, (donors, slots), 1)

    def fill(d):
        stage[d, 0:donors, 0:slots] = don[d].astype(F32)
        stage[d, donors : 2 * donors, 0:slots] = jnp.where(slot_id < live_s[0, d], wgt[d], 0.0)

    for d in range(n):
        fill(d)
    loads[0].wait()
    put_halo(0, psi0)

    pl.semaphore_wait(barrier, n - 1)
    halos = [halo_copies(s) for s in range(SWEEPS)]
    to_all(lambda dest: stage.at[dest], stage_in, stage_sem.at[0], stage_sem.at[1])
    for copy in halos[0]:
        copy.start()

    cells = jnp.concatenate(assemble(lambda d: recpad[d : d + 1, :]), axis=1)
    upper, lower = split_cell(cells)
    pick_hot[...] = (
        lax.broadcasted_iota(jnp.int32, (width, lists), 0) == lower
    ).astype(F32).astype(BF16)
    pick_block[...] = (lax.broadcasted_iota(jnp.int32, (blocks, lists), 0) == upper).astype(F32)
    pick(0, psi0)
    to_all(lambda dest: vsend.at[0, dest // per], vrecv.at[0], v_sem.at[0, 0], v_sem.at[0, 1])

    lane_of = lax.broadcasted_iota(jnp.int32, (8, LANES), 1)
    my_group = lax.rem(me, per)
    mine = (lane_of >= my_group * slots) & (lane_of < (my_group + 1) * slots)
    back = lax.rem((per - my_group) * slots, LANES)

    def couple(psi, sweep, faces, first):
        def chunk(c, carry):
            at = pl.ds(pl.multiple_of(c * LANES, LANES), LANES)
            values = [[near[f % 2, b, :, at] for b in range(nvar)] for f in faces]
            for a in range(nvar):
                total = rhs[a, :, at] if first else acc[a, :, at]
                for k, f in enumerate(faces):
                    for b in range(nvar):
                        total = total - jac[f, a, b, :, at].astype(F32) * values[k][b]
                acc[a, :, at] = total
            return carry

        lax.fori_loop(0, cols // LANES, chunk, 0)

    col_id = lax.broadcasted_iota(jnp.int32, (rows, cols), 1)
    row_id = lax.broadcasted_iota(jnp.int32, (rows, cols), 0)

    def sides(psi, sweep):
        for b in range(nvar):
            x = psi[b]
            near[0, b] = jnp.where(col_id == 0, 0.0, pltpu.roll(x, 1, 1))
            near[1, b] = jnp.where(col_id == cols - 1, 0.0, pltpu.roll(x, cols - 1, 1))

    def ends(psi, sweep):
        for copy in halos[sweep]:
            copy.wait_recv()
        for b in range(nvar):
            x = psi[b]
            low = jnp.where(me > 0, hrecv[sweep, 0, b : b + 1, :], 0.0)
            high = jnp.where(me < n - 1, hrecv[sweep, 1, b : b + 1, :], 0.0)
            near[0, b] = jnp.where(row_id == 0, low, pltpu.roll(x, 1, 0))
            near[1, b] = jnp.where(row_id == rows - 1, high, pltpu.roll(x, rows - 1, 0))

    def prepare_adds():
        wait_bytes(stage_in.at[pl.ds(0, n - 1)], stage_sem.at[1])
        stage_in[me] = stage[me]
        packed = jnp.concatenate(assemble(lambda s: stage_in[s]), axis=1)
        weights[...] = packed[donors : 2 * donors]
        for m in range(donors):
            upper, lower = split_cell(packed[m : m + 1])
            at = slice(m * lists, (m + 1) * lists)
            add_hot[:, at] = (
                lax.broadcasted_iota(jnp.int32, (width, lists), 0) == lower
            ).astype(F32).astype(BF16)
            add_block[m] = (
                lax.broadcasted_iota(jnp.int32, (blocks, lists), 0) == upper
            ).astype(F32)

    def add_donors(sweep):
        wait_bytes(vrecv.at[sweep, pl.ds(0, n - 1)], v_sem.at[sweep, 1])
        vrecv[sweep, me] = vsend[sweep, me // per]
        parts = assemble(lambda s: jnp.where(mine, vrecv[sweep, s], 0.0))
        values = jnp.concatenate([pltpu.roll(part, back, 1) for part in parts], axis=1)
        for m in range(donors):
            terms = values * weights[m : m + 1, :]
            pieces = two_pieces(terms)
            for k, piece in enumerate(pieces):
                piece = piece.astype(F32)
                for a in range(nvar):
                    at = k * full + a * blocks
                    lhs[at : at + blocks, m * lists : (m + 1) * lists] = (
                        add_block[m] * piece[a : a + 1, :]
                    ).astype(BF16)
        got = lax.dot_general(
            lhs[...], add_hot[...], (((1,), (1,)), ((), ())), preferred_element_type=F32
        )
        got = got[:full] + got[full:]
        for a in range(nvar):
            for q in range(strips):
                at = a * blocks + q * rows
                col = slice(q * width, (q + 1) * width)
                acc[a, :, col] = acc[a, :, col] + got[at : at + rows]

    def finish(psi, new):
        def chunk(c, total):
            at = pl.ds(pl.multiple_of(c * LANES, LANES), LANES)
            source = [acc[b, :, at] for b in range(nvar)]
            for a in range(nvar):
                value = dinv[a, 0, :, at] * source[0]
                for b in range(1, nvar):
                    value = value + dinv[a, b, :, at] * source[b]
                change = value - psi[a, :, at]
                total = total + change * change
                new[a, :, at] = value
            return total

        return lax.fori_loop(0, cols // LANES, chunk, jnp.zeros((rows, LANES), F32))

    sums = []
    psi = psi0
    for sweep in range(SWEEPS):
        new = out_ref if sweep == SWEEPS - 1 else psi1
        sides(psi, sweep)
        if sweep == 0:
            loads[4].wait()
            loads[5].wait()
        couple(psi, sweep, (2, 3), True)
        if sweep == 0:
            def square(c, total):
                at = pl.ds(pl.multiple_of(c * LANES, LANES), LANES)
                for a in range(nvar):
                    value = rhs[a, :, at]
                    total = total + value * value
                return total

            sums.append(
                lax.fori_loop(0, cols // LANES, square, jnp.zeros((rows, LANES), F32))
            )
            prepare_adds()
        ends(psi, sweep)
        couple(psi, sweep, (0, 1), False)
        add_donors(sweep)
        if sweep == 0:
            loads[6].wait()
        sums.append(finish(psi, new))
        psi = new
        if sweep + 1 < SWEEPS:
            pick(sweep + 1, psi)
            to_all(
                lambda dest: vsend.at[sweep + 1, dest // per],
                vrecv.at[sweep + 1],
                v_sem.at[sweep + 1, 0],
                v_sem.at[sweep + 1, 1],
            )
            put_halo(sweep + 1, psi)
            for copy in halos[sweep + 1]:
                copy.start()

    lines = [jnp.sum(s, axis=0, keepdims=True) for s in sums]
    lines.append(jnp.zeros((8 - len(lines), LANES), F32))
    nsend[...] = jnp.concatenate(lines, axis=0)
    to_all(lambda dest: nsend, nrecv, n_sem.at[0], n_sem.at[1])
    wait_bytes(stage_in.at[pl.ds(0, n - 1)], stage_sem.at[0])
    for sweep in range(SWEEPS):
        wait_bytes(vrecv.at[sweep, pl.ds(0, n - 1)], v_sem.at[sweep, 0])
        for copy in halos[sweep]:
            copy.wait_send()
    wait_bytes(nrecv.at[pl.ds(0, n - 1)], n_sem.at[1])
    nrecv[me] = nsend[...]
    total = nrecv[0]
    for s in range(1, n):
        total = total + nrecv[s]
    total = jnp.sum(total, axis=1, keepdims=True)
    result = jnp.sqrt(total[1 : 1 + SWEEPS] / (total[0:1] + 1e-6))
    for k in range(SWEEPS):
        norm_s[k] = result[k, 0]
    wait_bytes(nrecv.at[pl.ds(0, n - 1)], n_sem.at[0])


def body(n, right_side, adjoint_start, diag_inverse, face_jacobian, receptor, donor, weight, live):
    nvar, rows, cols = right_side.shape
    slots = receptor.shape[2]
    donors = donor.shape[2]
    lists = n * slots
    width = min(256, cols)
    blocks = rows * (cols // width)
    tiles = lists // LANES
    any_space = pl.BlockSpec(memory_space=pl.ANY)
    field = pltpu.VMEM((nvar, rows, cols), F32)
    adjoint, norms = pl.pallas_call(
        functools.partial(kernel, n),
        out_shape=(
            jax.ShapeDtypeStruct((nvar, rows, cols), F32),
            jax.ShapeDtypeStruct((SWEEPS,), F32),
        ),
        in_specs=[pl.BlockSpec(memory_space=pltpu.SMEM)] + [any_space] * 7,
        out_specs=(
            pl.BlockSpec(memory_space=pltpu.VMEM),
            pl.BlockSpec(memory_space=pltpu.SMEM),
        ),
        scratch_shapes=[
            field,
            field,
            field,
            pltpu.VMEM(diag_inverse.shape, F32),
            pltpu.VMEM(face_jacobian.shape, face_jacobian.dtype),
            pltpu.VMEM((n, slots), jnp.int32),
            pltpu.VMEM((n, donors, slots), jnp.int32),
            pltpu.VMEM((n, donors, slots), F32),
            field,
            pltpu.VMEM((2, nvar, rows, cols), F32),
            pltpu.VMEM((n, LANES), F32),
            pltpu.VMEM((n, 8, LANES), F32),
            pltpu.VMEM((n, 8, LANES), F32),
            pltpu.VMEM((SWEEPS, tiles, 8, LANES), F32),
            pltpu.VMEM((SWEEPS, n, 8, LANES), F32),
            pltpu.VMEM((SWEEPS, 2, nvar, cols), F32),
            pltpu.VMEM((SWEEPS, 2, nvar, cols), F32),
            pltpu.VMEM((8, LANES), F32),
            pltpu.VMEM((n, 8, LANES), F32),
            pltpu.VMEM((width, lists), BF16),
            pltpu.VMEM((blocks, lists), F32),
            pltpu.VMEM((width, donors * lists), BF16),
            pltpu.VMEM((donors, blocks, lists), F32),
            pltpu.VMEM((2 * nvar * blocks, donors * lists), BF16),
            pltpu.VMEM((donors, lists), F32),
            pltpu.SemaphoreType.DMA((7,)),
            pltpu.SemaphoreType.DMA((2,)),
            pltpu.SemaphoreType.DMA((SWEEPS, 2)),
            pltpu.SemaphoreType.DMA((SWEEPS, 2, 2)),
            pltpu.SemaphoreType.DMA((2,)),
        ],
        compiler_params=pltpu.CompilerParams(
            collective_id=0, has_side_effects=True, vmem_limit_bytes=60 * 1024 * 1024
        ),
    )(live, right_side, adjoint_start, diag_inverse, face_jacobian, receptor, donor, weight)
    return adjoint, norms


def solution(mesh):
    return jax.shard_map(
        functools.partial(body, mesh.shape["blk"]),
        mesh=mesh,
        in_specs=(
            P(None, ("design", "blk"), None),
            P(None, ("design", "blk"), None),
            P(None, None, ("design", "blk"), None),
            P(None, None, None, ("design", "blk"), None),
            P(("design", "blk"), None, None),
            P(("design", "blk"), None, None, None),
            P(("design", "blk"), None, None, None),
            P(("design", "blk"), None),
        ),
        out_specs=(P(None, ("design", "blk"), None), P("design")),
        check_vma=False,
    )
```

time: 104 us -> 27.1 us (0.26)
  blocking collectives: 30.1 us -> 0 us
  starting transfers between devices: 27.5 us -> 0 us
  Pallas kernels: 0 us -> 23.6 us
  other arithmetic: 16 us -> 0 us
  local copies, waits for them, and re-layouts: 13.7 us -> 2.75 us
  waiting for transfers between devices: 7.82 us -> 0 us
  matrix products: 6.72 us -> 0 us
    psum x1 -> x0, blocking collectives: 30.1 us -> none  [body(): totals = lax.psum(jnp.stack([rhs_local] + partials), 'blk')]
    pallas_call x0 -> x1, Pallas kernels: none -> 23.6 us  [body(): pl.pallas_call(functools.partial(kernel, n), out_shape=(jax.ShapeDtypeStr...]
    all_to_all x3 -> x0, starting transfers between devices: 20.4 us -> none  [the longest x2 12.9 us: body(): lax.all_to_all(weighted, 'blk', split_axis=1, concat_axis=1, tiled=True)]
    all_to_all x3 -> x0, waiting for transfers between devices: 7.81 us -> none  [the longest x2 7.81 us: body(): lax.all_to_all(weighted, 'blk', split_axis=1, concat_axis=1, tiled=True)]
    ppermute x4 -> x0, starting transfers between devices: 7.1 us -> none  [the longest x2 4.52 us: padded_2(): lax.ppermute(lax.slice_in_dim(block, block.shape[dim] - width, None, axis...]
    dot_general x4 -> x0, matrix products: 6.72 us -> none  [the longest x2 4.65 us: spread_one_group(): jnp.einsum('atb,to->abo', weighted, offset_hot, precision=lax.Precision.H...]
    another operation x6 -> x0, local copies, waits for them, and re-layouts: 5.06 us -> none  [the longest x2 2.61 us: pick_cells(): shaped = field.reshape(nvar, blocks, width)]
    unnamed x5 -> x0, other arithmetic: 3.18 us -> none
  transfers between devices with their start and end apart: 7 -> 0, of which waited for: 2 -> 0; matrix products, arithmetic and copies ran while one was open for 16% -> 0% of each run, Pallas kernels for 0% -> 0%
where the time goes in v1:
time: 27.1 us; the launch traced here: 27 us
  Pallas kernels  23.6 us (87%)
  local copies, waits for them, and re-layouts  2.75 us (10%)
  between operations  0.64 us (2%)
    pallas_call x1, Pallas kernels, body(): pl.pallas_call(functools.partial(kernel, n), out_shape=(jax.ShapeDtypeStr...  23.6 us
    unnamed x2, local copies, waits for them, and re-layouts  2.75 us

profile of v1, /device:TPU:0, one launch (start us, length us, event | category | flops | bytes accessed | tf_op | source)
XLA Modules:
  0.0 27.0 jit_solution(9402251328946611017)
XLA Ops:
  0.6 23.6 %shard_map.95 = (f32[6,8,1024]{2,1,0:T(8,128)}, f32[2]{0:T(128)}) custom-call(s32[1,16]{1,0:T(1,128)} %live_s.1, f32[6,8,1024]{2,1,0:T(8,128)} %rhs_h.1, f32[6,8,1024]{2,1,0:T(8,128)} %psi_h.1, f32[6,6,8,1024]{3,2,1,0:T(8,128)} %dinv_h.1, bf16[4,6,6,8,1024]{4,3,2,1,0:T(8,128)(2,1)} %jac_h.1, s32[1,16,16]{2,1,0:T(8,128)} %rec_h.1, s32[1,16,4,16]{3,2,1,0:T(4,128)} %don_h.1, ...), custom_call_target="tpu_custom_call" | custom-call | tf_op jit(solution)/shard_map/pallas_call | solution.py:372
  24.2 1.6 %copy.12 = f32[6,8,1024]{2,1,0:T(8,128)} copy(f32[6,8,1024]{2,1,0:T(8,128)} %get-tuple-element.4) | data formatting | bytes 393216
  25.8 1.1 %copy.13 = f32[2]{0:T(128)} copy(f32[2]{0:T(128)} %get-tuple-element.5) | data formatting | bytes 16

commit v2 on v1

--- a/solution.py
+++ b/solution.py
@@ -20,13 +20,27 @@
     return high, low
 
 
+def swap_groups(x, slots):
+    height, lanes = x.shape
+    row = lax.broadcasted_iota(jnp.int32, x.shape, 0)
+    lane = lax.broadcasted_iota(jnp.int32, x.shape, 1)
+    bit = 1
+    while bit < height:
+        step = bit * slots
+        differ = ((row * slots) ^ lane) & step
+        up = pltpu.roll(pltpu.roll(x, bit, 0), lanes - step, 1)
+        down = pltpu.roll(pltpu.roll(x, height - bit, 0), step, 1)
+        x = jnp.where(differ == 0, x, jnp.where((row & bit) != 0, up, down))
+        bit *= 2
+    return x
+
+
 def wait_bytes(ref, sem):
     pltpu.make_async_copy(ref, ref, sem).wait()
 
 
 def kernel(
     n,
-    live_s,
     rhs_h,
     psi_h,
     dinv_h,
@@ -34,8 +48,9 @@
     rec_h,
     don_h,
     wgt_h,
+    live_h,
     out_ref,
-    norm_s,
+    total_ref,
     rhs,
     psi0,
     psi1,
@@ -44,13 +59,15 @@
     rec,
     don,
     wgt,
+    live_s,
     acc,
     near,
     recpad,
     stage,
-    stage_in,
-    vsend,
-    vrecv,
+    first_out,
+    first_in,
+    later_out,
+    later_in,
     hsend,
     hrecv,
     nsend,
@@ -62,7 +79,6 @@
     lhs,
     weights,
     local_sem,
-    stage_sem,
     v_sem,
     h_sem,
     n_sem,
@@ -93,13 +109,14 @@
     loads = []
     for k, (src, dst) in enumerate(
         (
-            (psi_h, psi0),
             (rec_h.at[0], rec),
             (don_h.at[0], don),
             (wgt_h.at[0], wgt),
+            (psi_h, psi0),
             (jac_h, jac),
             (rhs_h, rhs),
             (dinv_h, dinv),
+            (live_h, live_s),
         )
     ):
         copy = pltpu.make_async_copy(src, dst, local_sem.at[k])
@@ -169,51 +186,47 @@
         )
         got = (got[:full] + got[full:]).reshape(nvar, blocks, lists)
         got = jnp.sum(got * pick_block[...][None], axis=1)
+        got = jnp.concatenate([got, jnp.zeros((per - nvar, lists), F32)], axis=0)
         for h in range(tiles):
-            vsend[sweep, h, 0:nvar, :] = got[:, h * LANES : (h + 1) * LANES]
+            packed = swap_groups(got[:, h * LANES : (h + 1) * LANES], slots)
+            if sweep == 0:
+                first_out[h * per : (h + 1) * per, 1, :] = packed
+            else:
+                later_out[sweep - 1, h * per : (h + 1) * per, 0, :] = packed
 
     stage[...] = jnp.zeros(stage.shape, F32)
     recpad[...] = jnp.zeros(recpad.shape, F32)
-    vsend[...] = jnp.zeros(vsend.shape, F32)
-    loads[1].wait()
+    loads[0].wait()
     recpad[:, 0:slots] = rec[...].astype(F32)
-    loads[2].wait()
-    loads[3].wait()
-    slot_id = lax.broadcasted_iota(jnp.int32, (donors, slots), 1)
-
-    def fill(d):
-        stage[d, 0:donors, 0:slots] = don[d].astype(F32)
-        stage[d, donors : 2 * donors, 0:slots] = jnp.where(slot_id < live_s[0, d], wgt[d], 0.0)
-
-    for d in range(n):
-        fill(d)
-    loads[0].wait()
-    put_halo(0, psi0)
-
-    pl.semaphore_wait(barrier, n - 1)
-    halos = [halo_copies(s) for s in range(SWEEPS)]
-    to_all(lambda dest: stage.at[dest], stage_in, stage_sem.at[0], stage_sem.at[1])
-    for copy in halos[0]:
-        copy.start()
-
     cells = jnp.concatenate(assemble(lambda d: recpad[d : d + 1, :]), axis=1)
     upper, lower = split_cell(cells)
     pick_hot[...] = (
         lax.broadcasted_iota(jnp.int32, (width, lists), 0) == lower
     ).astype(F32).astype(BF16)
     pick_block[...] = (lax.broadcasted_iota(jnp.int32, (blocks, lists), 0) == upper).astype(F32)
+    loads[1].wait()
+    loads[2].wait()
+    loads[7].wait()
+    slot_id = lax.broadcasted_iota(jnp.int32, (donors, slots), 1)
+    for d in range(n):
+        stage[d, 0:donors, 0:slots] = don[d].astype(F32)
+        stage[d, donors : 2 * donors, 0:slots] = jnp.where(slot_id < live_s[0, d], wgt[d], 0.0)
+    for h, part in enumerate(assemble(lambda d: stage[d])):
+        first_out[h * per : (h + 1) * per, 0, :] = swap_groups(part, slots)
+    loads[3].wait()
+    put_halo(0, psi0)
     pick(0, psi0)
-    to_all(lambda dest: vsend.at[0, dest // per], vrecv.at[0], v_sem.at[0, 0], v_sem.at[0, 1])
-
-    lane_of = lax.broadcasted_iota(jnp.int32, (8, LANES), 1)
-    my_group = lax.rem(me, per)
-    mine = (lane_of >= my_group * slots) & (lane_of < (my_group + 1) * slots)
-    back = lax.rem((per - my_group) * slots, LANES)
+
+    pl.semaphore_wait(barrier, n - 1)
+    halos = [halo_copies(s) for s in range(SWEEPS)]
+    to_all(lambda dest: first_out.at[dest], first_in, v_sem.at[0, 0], v_sem.at[0, 1])
+    for copy in halos[0]:
+        copy.start()
 
     def couple(psi, sweep, faces, first):
         def chunk(c, carry):
             at = pl.ds(pl.multiple_of(c * LANES, LANES), LANES)
-            values = [[near[f % 2, b, :, at] for b in range(nvar)] for f in faces]
+            values = [[near[f, b, :, at] for b in range(nvar)] for f in faces]
             for a in range(nvar):
                 total = rhs[a, :, at] if first else acc[a, :, at]
                 for k, f in enumerate(faces):
@@ -230,8 +243,8 @@
     def sides(psi, sweep):
         for b in range(nvar):
             x = psi[b]
-            near[0, b] = jnp.where(col_id == 0, 0.0, pltpu.roll(x, 1, 1))
-            near[1, b] = jnp.where(col_id == cols - 1, 0.0, pltpu.roll(x, cols - 1, 1))
+            near[2, b] = jnp.where(col_id == 0, 0.0, pltpu.roll(x, 1, 1))
+            near[3, b] = jnp.where(col_id == cols - 1, 0.0, pltpu.roll(x, cols - 1, 1))
 
     def ends(psi, sweep):
         for copy in halos[sweep]:
@@ -244,9 +257,15 @@
             near[1, b] = jnp.where(row_id == rows - 1, high, pltpu.roll(x, rows - 1, 0))
 
     def prepare_adds():
-        wait_bytes(stage_in.at[pl.ds(0, n - 1)], stage_sem.at[1])
-        stage_in[me] = stage[me]
-        packed = jnp.concatenate(assemble(lambda s: stage_in[s]), axis=1)
+        wait_bytes(first_in.at[pl.ds(0, n - 1)], v_sem.at[0, 1])
+        first_in[me] = first_out[me]
+        packed = jnp.concatenate(
+            [
+                swap_groups(first_in[h * per : (h + 1) * per, 0, :], slots)
+                for h in range(tiles)
+            ],
+            axis=1,
+        )
         weights[...] = packed[donors : 2 * donors]
         for m in range(donors):
             upper, lower = split_cell(packed[m : m + 1])
@@ -259,10 +278,15 @@
             ).astype(F32)
 
     def add_donors(sweep):
-        wait_bytes(vrecv.at[sweep, pl.ds(0, n - 1)], v_sem.at[sweep, 1])
-        vrecv[sweep, me] = vsend[sweep, me // per]
-        parts = assemble(lambda s: jnp.where(mine, vrecv[sweep, s], 0.0))
-        values = jnp.concatenate([pltpu.roll(part, back, 1) for part in parts], axis=1)
+        if sweep == 0:
+            parts = [first_in[h * per : (h + 1) * per, 1, :] for h in range(tiles)]
+        else:
+            wait_bytes(later_in.at[sweep - 1, pl.ds(0, n - 1)], v_sem.at[sweep, 1])
+            later_in[sweep - 1, me] = later_out[sweep - 1, me]
+            parts = [
+                later_in[sweep - 1, h * per : (h + 1) * per, 0, :] for h in range(tiles)
+            ]
+        values = jnp.concatenate([swap_groups(part, slots) for part in parts], axis=1)
         for m in range(donors):
             terms = values * weights[m : m + 1, :]
             pieces = two_pieces(terms)
@@ -329,8 +353,8 @@
         if sweep + 1 < SWEEPS:
             pick(sweep + 1, psi)
             to_all(
-                lambda dest: vsend.at[sweep + 1, dest // per],
-                vrecv.at[sweep + 1],
+                lambda dest: later_out.at[sweep, dest],
+                later_in.at[sweep],
                 v_sem.at[sweep + 1, 0],
                 v_sem.at[sweep + 1, 1],
             )
@@ -338,13 +362,19 @@
             for copy in halos[sweep + 1]:
                 copy.start()
 
-    lines = [jnp.sum(s, axis=0, keepdims=True) for s in sums]
-    lines.append(jnp.zeros((8 - len(lines), LANES), F32))
-    nsend[...] = jnp.concatenate(lines, axis=0)
+    lane = lax.broadcasted_iota(jnp.int32, (1, LANES), 1)
+    row = jnp.zeros((1, LANES), F32)
+    for q, part in enumerate(sums):
+        line = jnp.sum(part, axis=0, keepdims=True)
+        line = line + pltpu.roll(line, 64, 1)
+        line = line + pltpu.roll(line, 32, 1)
+        row = jnp.where((lane >= 32 * q) & (lane < 32 * (q + 1)), line, row)
+    nsend[...] = row
     to_all(lambda dest: nsend, nrecv, n_sem.at[0], n_sem.at[1])
-    wait_bytes(stage_in.at[pl.ds(0, n - 1)], stage_sem.at[0])
+    wait_bytes(first_in.at[pl.ds(0, n - 1)], v_sem.at[0, 0])
     for sweep in range(SWEEPS):
-        wait_bytes(vrecv.at[sweep, pl.ds(0, n - 1)], v_sem.at[sweep, 0])
+        if sweep:
+            wait_bytes(later_in.at[sweep - 1, pl.ds(0, n - 1)], v_sem.at[sweep, 0])
         for copy in halos[sweep]:
             copy.wait_send()
     wait_bytes(nrecv.at[pl.ds(0, n - 1)], n_sem.at[1])
@@ -352,11 +382,25 @@
     total = nrecv[0]
     for s in range(1, n):
         total = total + nrecv[s]
-    total = jnp.sum(total, axis=1, keepdims=True)
-    result = jnp.sqrt(total[1 : 1 + SWEEPS] / (total[0:1] + 1e-6))
+    total_ref[...] = total
+    wait_bytes(nrecv.at[pl.ds(0, n - 1)], n_sem.at[0])
+
+
+def close(adjoint_ref, total_ref, out_h, norm_s, sem):
+    copy = pltpu.make_async_copy(adjoint_ref, out_h, sem)
+    copy.start()
+    lane = lax.broadcasted_iota(jnp.int32, (1, LANES), 1)
+    total = total_ref[...]
+    sums = [
+        jnp.sum(
+            jnp.where((lane >= 32 * q) & (lane < 32 * (q + 1)), total, 0.0), axis=1, keepdims=True
+        )
+        for q in range(SWEEPS + 1)
+    ]
     for k in range(SWEEPS):
-        norm_s[k] = result[k, 0]
-    wait_bytes(nrecv.at[pl.ds(0, n - 1)], n_sem.at[0])
+        result = jnp.sqrt(sums[k + 1] / (sums[0] + 1e-6))
+        norm_s[k] = result[0, 0]
+    copy.wait()
 
 
 def body(n, right_side, adjoint_start, diag_inverse, face_jacobian, receptor, donor, weight, live):
@@ -366,19 +410,31 @@
     lists = n * slots
     width = min(256, cols)
     blocks = rows * (cols // width)
-    tiles = lists // LANES
     any_space = pl.BlockSpec(memory_space=pl.ANY)
     field = pltpu.VMEM((nvar, rows, cols), F32)
-    adjoint, norms = pl.pallas_call(
+    placed = [
+        pltpu.with_memory_space_constraint(x, pltpu.HBM)
+        for x in (
+            right_side,
+            adjoint_start,
+            diag_inverse,
+            face_jacobian,
+            receptor,
+            donor,
+            weight,
+            live,
+        )
+    ]
+    adjoint, total = pl.pallas_call(
         functools.partial(kernel, n),
         out_shape=(
             jax.ShapeDtypeStruct((nvar, rows, cols), F32),
-            jax.ShapeDtypeStruct((SWEEPS,), F32),
+            jax.ShapeDtypeStruct((1, LANES), F32),
         ),
-        in_specs=[pl.BlockSpec(memory_space=pltpu.SMEM)] + [any_space] * 7,
+        in_specs=[pl.BlockSpec(memory_space=pltpu.HBM)] * 8,
         out_specs=(
             pl.BlockSpec(memory_space=pltpu.VMEM),
-            pl.BlockSpec(memory_space=pltpu.SMEM),
+            pl.BlockSpec(memory_space=pltpu.VMEM),
         ),
         scratch_shapes=[
             field,
@@ -389,34 +445,45 @@
             pltpu.VMEM((n, slots), jnp.int32),
             pltpu.VMEM((n, donors, slots), jnp.int32),
             pltpu.VMEM((n, donors, slots), F32),
+            pltpu.SMEM((1, n), jnp.int32),
             field,
-            pltpu.VMEM((2, nvar, rows, cols), F32),
+            pltpu.VMEM((4, nvar, rows, cols), F32),
             pltpu.VMEM((n, LANES), F32),
-            pltpu.VMEM((n, 8, LANES), F32),
-            pltpu.VMEM((n, 8, LANES), F32),
-            pltpu.VMEM((SWEEPS, tiles, 8, LANES), F32),
-            pltpu.VMEM((SWEEPS, n, 8, LANES), F32),
+            pltpu.VMEM((n, 2 * donors, LANES), F32),
+            pltpu.VMEM((n, 2, LANES), F32),
+            pltpu.VMEM((n, 2, LANES), F32),
+            pltpu.VMEM((SWEEPS - 1, n, 1, LANES), F32),
+            pltpu.VMEM((SWEEPS - 1, n, 1, LANES), F32),
             pltpu.VMEM((SWEEPS, 2, nvar, cols), F32),
             pltpu.VMEM((SWEEPS, 2, nvar, cols), F32),
-            pltpu.VMEM((8, LANES), F32),
-            pltpu.VMEM((n, 8, LANES), F32),
+            pltpu.VMEM((1, LANES), F32),
+            pltpu.VMEM((n, 1, LANES), F32),
             pltpu.VMEM((width, lists), BF16),
             pltpu.VMEM((blocks, lists), F32),
             pltpu.VMEM((width, donors * lists), BF16),
             pltpu.VMEM((donors, blocks, lists), F32),
             pltpu.VMEM((2 * nvar * blocks, donors * lists), BF16),
             pltpu.VMEM((donors, lists), F32),
-            pltpu.SemaphoreType.DMA((7,)),
-            pltpu.SemaphoreType.DMA((2,)),
+            pltpu.SemaphoreType.DMA((8,)),
             pltpu.SemaphoreType.DMA((SWEEPS, 2)),
             pltpu.SemaphoreType.DMA((SWEEPS, 2, 2)),
             pltpu.SemaphoreType.DMA((2,)),
         ],
         compiler_params=pltpu.CompilerParams(
-            collective_id=0, has_side_effects=True, vmem_limit_bytes=60 * 1024 * 1024
+            collective_id=0, has_side_effects=True, vmem_limit_bytes=36 * 1024 * 1024
         ),
-    )(live, right_side, adjoint_start, diag_inverse, face_jacobian, receptor, donor, weight)
-    return adjoint, norms
+    )(*placed)
+    return pl.pallas_call(
+        close,
+        out_shape=(
+            jax.ShapeDtypeStruct((nvar, rows, cols), F32),
+            jax.ShapeDtypeStruct((SWEEPS,), F32),
+        ),
+        in_specs=[pl.BlockSpec(memory_space=pltpu.VMEM)] * 2,
+        out_specs=(any_space, pl.BlockSpec(memory_space=pltpu.SMEM)),
+        scratch_shapes=[pltpu.SemaphoreType.DMA],
+        compiler_params=pltpu.CompilerParams(vmem_limit_bytes=8 * 1024 * 1024),
+    )(adjoint, total)
 
 
 def solution(mesh):

time: 27.1 us -> 23.5 us (0.87)
  local copies, waits for them, and re-layouts: 2.75 us -> 0 us
  Pallas kernels: 23.6 us -> 22.6 us
    unnamed x2 -> x0, local copies, waits for them, and re-layouts: 2.75 us -> none
    pallas_call x1, Pallas kernels: 23.6 us -> 21.4 us  [body(): pl.pallas_call(functools.partial(kernel, n), out_shape=(jax.ShapeDtypeStr...]
    pallas_call x0 -> x1, Pallas kernels: none -> 1.2 us  [body(): pl.pallas_call(close, out_shape=(jax.ShapeDtypeStruct((nvar, rows, cols),...]
where the time goes in v2:
time: 23.5 us; the launch traced here: 23.3 us
  Pallas kernels  22.6 us (96%)
  between operations  0.64 us (3%)
    pallas_call x1, Pallas kernels, body(): pl.pallas_call(functools.partial(kernel, n), out_shape=(jax.ShapeDtypeStr...  21.4 us
    pallas_call x1, Pallas kernels, body(): pl.pallas_call(close, out_shape=(jax.ShapeDtypeStruct((nvar, rows, cols),...  1.2 us

profile of v2, /device:TPU:0, one launch (start us, length us, event | category | flops | bytes accessed | tf_op | source)
XLA Modules:
  0.0 23.3 jit_solution(15829582261832239526)
XLA Ops:
  0.6 21.4 %shard_map.95 = (f32[6,8,1024]{2,1,0:T(8,128)S(1)}, f32[1,128]{1,0:T(1,128)S(1)}) custom-call(f32[6,8,1024]{2,1,0:T(8,128)} %rhs_h.1, f32[6,8,1024]{2,1,0:T(8,128)} %psi_h.1, f32[6,6,8,1024]{3,2,1,0:T(8,128)} %dinv_h.1, bf16[4,6,6,8,1024]{4,3,2,1,0:T(8,128)(2,1)} %jac_h.1, s32[1,16,16]{2,1,0:T(8,128)} %rec_h.1, s32[1,16,4,16]{3,2,1,0:T(4,128)} %don_h.1, ...), custom_call_target="tpu_custom_call" | custom-call | tf_op jit(solution)/shard_map/pallas_call | solution.py:428
  22.1 1.2 %shard_map.96 = (f32[6,8,1024]{2,1,0:T(8,128)}, f32[2]{0:T(128)}) custom-call(f32[6,8,1024]{2,1,0:T(8,128)S(1)} %get-tuple-element.4.adjoint_ref, f32[1,128]{1,0:T(1,128)S(1)} %get-tuple-element.5.total_ref), custom_call_target="tpu_custom_call" | custom-call | tf_op jit(solution)/shard_map/pallas_call | solution.py:476

commit v3 on v2

--- a/solution.py
+++ b/solution.py
@@ -96,15 +96,22 @@
     me = lax.axis_index("blk")
     design = lax.axis_index("design")
 
+    mirrored = me < n // 2
+    place = jnp.where(mirrored, n - 1 - me, me)
+
+    def partner(k):
+        other = jnp.where(k >= place, k + 1, k)
+        return jnp.where(mirrored, n - 1 - other, other)
+
     barrier = pltpu.get_barrier_semaphore()
 
-    def greet(j, carry):
+    def greet(k, carry):
         pl.semaphore_signal(
-            barrier, inc=1, device_id=(design, lax.rem(me + j, n)), device_id_type=MESH
+            barrier, inc=1, device_id=(design, partner(k)), device_id_type=MESH
         )
         return carry
 
-    lax.fori_loop(1, n, greet, 0)
+    lax.fori_loop(0, n - 1, greet, 0)
 
     loads = []
     for k, (src, dst) in enumerate(
@@ -130,8 +137,8 @@
         return (q * rows + i).astype(jnp.int32), (j - q * width).astype(jnp.int32)
 
     def to_all(source_of, dest_ref, send_sem, recv_sem):
-        def send(j, carry):
-            dest = lax.rem(me + j, n)
+        def send(k, carry):
+            dest = partner(k)
             pltpu.make_async_remote_copy(
                 src_ref=source_of(dest),
                 dst_ref=dest_ref.at[me],
@@ -142,7 +149,7 @@
             ).start()
             return carry
 
-        lax.fori_loop(1, n, send, 0)
+        lax.fori_loop(0, n - 1, send, 0)
 
     def halo_copies(sweep):
         below = lax.rem(me + n - 1, n)
@@ -151,8 +158,8 @@
             pltpu.make_async_remote_copy(
                 src_ref=hsend.at[sweep, side],
                 dst_ref=hrecv.at[sweep, side],
-                send_sem=h_sem.at[sweep, side, 0],
-                recv_sem=h_sem.at[sweep, side, 1],
+                send_sem=h_sem.at[sweep, 0],
+                recv_sem=h_sem.at[sweep, 1],
                 device_id=(design, target),
                 device_id_type=MESH,
             )
@@ -235,7 +242,7 @@
                 acc[a, :, at] = total
             return carry
 
-        lax.fori_loop(0, cols // LANES, chunk, 0)
+        lax.fori_loop(0, cols // LANES, chunk, 0, unroll=2)
 
     col_id = lax.broadcasted_iota(jnp.int32, (rows, cols), 1)
     row_id = lax.broadcasted_iota(jnp.int32, (rows, cols), 0)
@@ -247,8 +254,7 @@
             near[3, b] = jnp.where(col_id == cols - 1, 0.0, pltpu.roll(x, cols - 1, 1))
 
     def ends(psi, sweep):
-        for copy in halos[sweep]:
-            copy.wait_recv()
+        wait_bytes(hrecv.at[sweep], h_sem.at[sweep, 1])
         for b in range(nvar):
             x = psi[b]
             low = jnp.where(me > 0, hrecv[sweep, 0, b : b + 1, :], 0.0)
@@ -320,7 +326,7 @@
                 new[a, :, at] = value
             return total
 
-        return lax.fori_loop(0, cols // LANES, chunk, jnp.zeros((rows, LANES), F32))
+        return lax.fori_loop(0, cols // LANES, chunk, jnp.zeros((rows, LANES), F32), unroll=2)
 
     sums = []
     psi = psi0
@@ -340,11 +346,12 @@
                 return total
 
             sums.append(
-                lax.fori_loop(0, cols // LANES, square, jnp.zeros((rows, LANES), F32))
+                lax.fori_loop(0, cols // LANES, square, jnp.zeros((rows, LANES), F32), unroll=2)
             )
-            prepare_adds()
         ends(psi, sweep)
         couple(psi, sweep, (0, 1), False)
+        if sweep == 0:
+            prepare_adds()
         add_donors(sweep)
         if sweep == 0:
             loads[6].wait()
@@ -375,8 +382,7 @@
     for sweep in range(SWEEPS):
         if sweep:
             wait_bytes(later_in.at[sweep - 1, pl.ds(0, n - 1)], v_sem.at[sweep, 0])
-        for copy in halos[sweep]:
-            copy.wait_send()
+        wait_bytes(hsend.at[sweep], h_sem.at[sweep, 0])
     wait_bytes(nrecv.at[pl.ds(0, n - 1)], n_sem.at[1])
     nrecv[me] = nsend[...]
     total = nrecv[0]
@@ -386,8 +392,8 @@
     wait_bytes(nrecv.at[pl.ds(0, n - 1)], n_sem.at[0])
 
 
-def close(adjoint_ref, total_ref, out_h, norm_s, sem):
-    copy = pltpu.make_async_copy(adjoint_ref, out_h, sem)
+def close(adjoint_ref, total_ref, out_h, norm_h, norm_s, sem):
+    copy = pltpu.make_async_copy(adjoint_ref, out_h, sem.at[0])
     copy.start()
     lane = lax.broadcasted_iota(jnp.int32, (1, LANES), 1)
     total = total_ref[...]
@@ -400,7 +406,10 @@
     for k in range(SWEEPS):
         result = jnp.sqrt(sums[k + 1] / (sums[0] + 1e-6))
         norm_s[k] = result[0, 0]
+    last = pltpu.make_async_copy(norm_s, norm_h, sem.at[1])
+    last.start()
     copy.wait()
+    last.wait()
 
 
 def body(n, right_side, adjoint_start, diag_inverse, face_jacobian, receptor, donor, weight, live):
@@ -466,7 +475,7 @@
             pltpu.VMEM((donors, lists), F32),
             pltpu.SemaphoreType.DMA((8,)),
             pltpu.SemaphoreType.DMA((SWEEPS, 2)),
-            pltpu.SemaphoreType.DMA((SWEEPS, 2, 2)),
+            pltpu.SemaphoreType.DMA((SWEEPS, 2)),
             pltpu.SemaphoreType.DMA((2,)),
         ],
         compiler_params=pltpu.CompilerParams(
@@ -480,8 +489,8 @@
             jax.ShapeDtypeStruct((SWEEPS,), F32),
         ),
         in_specs=[pl.BlockSpec(memory_space=pltpu.VMEM)] * 2,
-        out_specs=(any_space, pl.BlockSpec(memory_space=pltpu.SMEM)),
-        scratch_shapes=[pltpu.SemaphoreType.DMA],
+        out_specs=(any_space, any_space),
+        scratch_shapes=[pltpu.SMEM((SWEEPS,), F32), pltpu.SemaphoreType.DMA((2,))],
         compiler_params=pltpu.CompilerParams(vmem_limit_bytes=8 * 1024 * 1024),
     )(adjoint, total)
 

time: 23.5 us -> 22.3 us (0.949)
  Pallas kernels: 22.6 us -> 21.4 us
    pallas_call x1, Pallas kernels: 21.4 us -> 20.7 us  [body(): pl.pallas_call(functools.partial(kernel, n), out_shape=(jax.ShapeDtypeStr...]
    pallas_call x1, Pallas kernels: 1.2 us -> 0.71 us  [body(): pl.pallas_call(close, out_shape=(jax.ShapeDtypeStruct((nvar, rows, cols),...]
where the time goes in v3:
time: 22.3 us; the launch traced here: 22.1 us
  Pallas kernels  21.4 us (96%)
  between operations  0.64 us (3%)
    pallas_call x1, Pallas kernels, body(): pl.pallas_call(functools.partial(kernel, n), out_shape=(jax.ShapeDtypeStr...  20.7 us
    pallas_call x1, Pallas kernels, body(): pl.pallas_call(close, out_shape=(jax.ShapeDtypeStruct((nvar, rows, cols),...  0.71 us

profile of v3, /device:TPU:0, one launch (start us, length us, event | category | flops | bytes accessed | tf_op | source)
XLA Modules:
  0.0 22.1 jit_solution(9824890927280506788)
XLA Ops:
  0.6 20.7 %shard_map.95 = (f32[6,8,1024]{2,1,0:T(8,128)S(1)}, f32[1,128]{1,0:T(1,128)S(1)}) custom-call(f32[6,8,1024]{2,1,0:T(8,128)} %rhs_h.1, f32[6,8,1024]{2,1,0:T(8,128)} %psi_h.1, f32[6,6,8,1024]{3,2,1,0:T(8,128)} %dinv_h.1, bf16[4,6,6,8,1024]{4,3,2,1,0:T(8,128)(2,1)} %jac_h.1, s32[1,16,16]{2,1,0:T(8,128)} %rec_h.1, s32[1,16,4,16]{3,2,1,0:T(4,128)} %don_h.1, ...), custom_call_target="tpu_custom_call" | custom-call | tf_op jit(solution)/shard_map/pallas_call | solution.py:437
  21.4 0.7 %shard_map.96 = (f32[6,8,1024]{2,1,0:T(8,128)}, f32[2]{0:T(128)}) custom-call(f32[6,8,1024]{2,1,0:T(8,128)S(1)} %get-tuple-element.4.adjoint_ref, f32[1,128]{1,0:T(1,128)S(1)} %get-tuple-element.5.total_ref), custom_call_target="tpu_custom_call" | custom-call | tf_op jit(solution)/shard_map/pallas_call | solution.py:485

commit v4 on v3

--- a/solution.py
+++ b/solution.py
@@ -326,7 +326,7 @@
                 new[a, :, at] = value
             return total
 
-        return lax.fori_loop(0, cols // LANES, chunk, jnp.zeros((rows, LANES), F32), unroll=2)
+        return lax.fori_loop(0, cols // LANES, chunk, jnp.zeros((rows, LANES), F32), unroll=True)
 
     sums = []
     psi = psi0

time: 22.3 us -> 21.9 us (0.982)
  Pallas kernels: 21.4 us -> 21.1 us
    pallas_call x1, Pallas kernels: 20.7 us -> 20.4 us  [body(): pl.pallas_call(functools.partial(kernel, n), out_shape=(jax.ShapeDtypeStr...]
where the time goes in v4:
time: 21.9 us; the launch traced here: 21.7 us
  Pallas kernels  21.1 us (96%)
  between operations  0.64 us (3%)
    pallas_call x1, Pallas kernels, body(): pl.pallas_call(functools.partial(kernel, n), out_shape=(jax.ShapeDtypeStr...  20.4 us
    pallas_call x1, Pallas kernels, body(): pl.pallas_call(close, out_shape=(jax.ShapeDtypeStruct((nvar, rows, cols),...  0.71 us

profile of v4, /device:TPU:0, one launch (start us, length us, event | category | flops | bytes accessed | tf_op | source)
XLA Modules:
  0.0 21.7 jit_solution(12636675106180238256)
XLA Ops:
  0.6 20.4 %shard_map.95 = (f32[6,8,1024]{2,1,0:T(8,128)S(1)}, f32[1,128]{1,0:T(1,128)S(1)}) custom-call(f32[6,8,1024]{2,1,0:T(8,128)} %rhs_h.1, f32[6,8,1024]{2,1,0:T(8,128)} %psi_h.1, f32[6,6,8,1024]{3,2,1,0:T(8,128)} %dinv_h.1, bf16[4,6,6,8,1024]{4,3,2,1,0:T(8,128)(2,1)} %jac_h.1, s32[1,16,16]{2,1,0:T(8,128)} %rec_h.1, s32[1,16,4,16]{3,2,1,0:T(4,128)} %don_h.1, ...), custom_call_target="tpu_custom_call" | custom-call | tf_op jit(solution)/shard_map/pallas_call | solution.py:437
  21.0 0.7 %shard_map.96 = (f32[6,8,1024]{2,1,0:T(8,128)}, f32[2]{0:T(128)}) custom-call(f32[6,8,1024]{2,1,0:T(8,128)S(1)} %get-tuple-element.4.adjoint_ref, f32[1,128]{1,0:T(1,128)S(1)} %get-tuple-element.5.total_ref), custom_call_target="tpu_custom_call" | custom-call | tf_op jit(solution)/shard_map/pallas_call | solution.py:485
